TPU v7x, 32 devices: a whole 2x2x4 slice. The times are simulated.
32 devices in a mesh: rep: 2 (over x), tp: 4 (over z), dp: 4 (over y, core).
Axes of the slice: x: 2, y: 2, z: 4, core: 2. Of those that a mesh axis runs over, the one named last changes fastest.
Arguments:
- grad_partial: float32 [8, 8, 768, 3072], P(('rep', 'dp'), None, None, 'tp'), parts along dimension 0
- momentum: float32 [16, 768, 3072], P('rep', 'dp', 'tp'), parts along dimension 0
- weight: float32 [16, 768, 3072], P('rep', 'dp', 'tp'), parts along dimension 0
- learn_rate: float32 [16], P('rep'), parts along dimension 0
- decay_rate: float32 [], replicated
Outputs:
- output 1: float32 [16, 768, 3072], P('rep', 'dp', 'tp'), parts along dimension 0
- output 2: float32 [16, 768, 3072], P('rep', 'dp', 'tp'), parts along dimension 0
- output 3: bfloat16 [16, 768, 3072], P('rep', None, 'tp'), parts along dimension 0
There are 2 independent parts. A program takes and returns all parts, laid end to end along the dimension named above; an argument that names none is the same for every part.
All inputs are finite; a program needn't handle non-finite values.
Results may differ from a plain program's by a relative error of at most 0.0113773.
Values are sent between devices in bfloat16 or wider.
A program may use at most 1 GiB of HBM per device.

v0:
```python
import math
import jax
import jax.numpy as jnp
from jax import lax
from jax.sharding import PartitionSpec as P, NamedSharding

MOMENTUM = 0.95
NS_STEPS = 5
COEF_A = 3.4445
COEF_B = -4.7750
COEF_C = 2.0315
NORM_EPS = 1e-7


def newton_schulz(update, short_rows):
    upd_f32 = update.astype(jnp.float32)
    norm_val = jnp.sqrt(jnp.sum(upd_f32 * upd_f32, axis=(1, 2), keepdims=True))
    x_cur = (upd_f32 / (norm_val + NORM_EPS)).astype(jnp.bfloat16)
    for step_idx in range(NS_STEPS):
        if short_rows:
            gram_mat = jnp.einsum("bik,bjk->bij", x_cur, x_cur, preferred_element_type=jnp.float32)
        else:
            gram_mat = jnp.einsum("bki,bkj->bij", x_cur, x_cur, preferred_element_type=jnp.float32)
        gram_mat = gram_mat.astype(jnp.bfloat16)
        gram_sq = jnp.einsum("bij,bjk->bik", gram_mat, gram_mat, preferred_element_type=jnp.float32)
        poly_mat = (COEF_B * gram_mat.astype(jnp.float32) + COEF_C * gram_sq).astype(jnp.bfloat16)
        if short_rows:
            prod_mat = jnp.einsum("bij,bjk->bik", poly_mat, x_cur, preferred_element_type=jnp.float32)
        else:
            prod_mat = jnp.einsum("bkj,bij->bki", x_cur, poly_mat, preferred_element_type=jnp.float32)
        x_cur = (COEF_A * x_cur.astype(jnp.float32) + prod_mat).astype(jnp.bfloat16)
    return x_cur


def solution(mesh):
    dp_size = mesh.shape["dp"]
    tp_size = mesh.shape["tp"]

    def local_step(grad_local, mom_local, weight_local, learn_rate, decay_rate):
        grad_sum = lax.psum_scatter(grad_local[0], "dp", scatter_dimension=1, tiled=True)
        grad_mean = grad_sum / dp_size
        mom_new = MOMENTUM * mom_local + grad_mean
        update = (grad_mean + MOMENTUM * mom_new).astype(jnp.bfloat16)
        whole_rows = lax.all_to_all(update, "dp", split_axis=0, concat_axis=1, tiled=True)
        whole_mats = lax.all_gather(whole_rows, "tp", axis=2, tiled=True)
        row_count = whole_mats.shape[1]
        col_count = whole_mats.shape[2]
        ortho_mat = newton_schulz(whole_mats, row_count <= col_count)
        col_width = col_count // tp_size
        own_cols = lax.dynamic_slice_in_dim(ortho_mat, lax.axis_index("tp") * col_width, col_width, axis=2)
        ortho_rows = lax.all_to_all(own_cols, "dp", split_axis=1, concat_axis=0, tiled=True)
        out_scale = 0.2 * math.sqrt(max(row_count, col_count))
        rate_col = learn_rate[:, None, None]
        weight_new = weight_local - rate_col * (out_scale * ortho_rows.astype(jnp.float32) + decay_rate * weight_local)
        weight_full = lax.all_gather(weight_new.astype(jnp.bfloat16), "dp", axis=1, tiled=True)
        return mom_new, weight_new, weight_full

    return jax.shard_map(
        local_step,
        mesh=mesh,
        in_specs=(P(("rep", "dp"), None, None, "tp"), P("rep", "dp", "tp"), P("rep", "dp", "tp"), P("rep"), P()),
        out_specs=(P("rep", "dp", "tp"), P("rep", "dp", "tp"), P("rep", None, "tp")),
        check_vma=False,
    )
```

profile of v0, /device:TPU:11, one launch (start us, length us, event | category | flops | bytes accessed | tf_op | source)
XLA Modules:
  0.0 637.9 jit_solution(4641476432401675224)
XLA Ops:
  7.2 0.0 reduce-scatter.2.cloned.1.call-start
  7.2 0.7 reduce-scatter.2.cloned.1.call-update
  7.9 0.0 all-gather.3.cloned.1.call-start
  7.9 140.5 %reduce-scatter.2.cloned.1.call-done = f32[8,192,768]{2,1,0:T(8,128)} async-done(((f32[8,768,768]{2,1,0:T(8,128)}), f32[8,192,768]{2,1,0:T(8,128)}) %reduce-scatter.2.cloned.1.call-update) | async-done | bytes 4718608 | tf_op jit(solution)/shard_map/reduce_scatter | solution.py:40
  148.5 7.0 %add_convert_fusion.9 = (bf16[8,192,768]{2,1,0:T(8,128)(2,1)S(1)}, f32[8,192,768]{2,1,0:T(8,128)}) fusion(f32[8,192,768]{2,1,0:T(8,128)} %reduce-scatter.2.cloned.1.call-done, f32[8,192,768]{2,1,0:T(8,128)} %param.6), kind=kLoop, calls=%fused_computation.19 | loop fusion | flops 7077888 | bytes 16515072 | tf_op jit(solution)/shard_map/convert_element_type | solution.py:43
  155.4 30.8 %all_to_all.27 = bf16[8,192,768]{2,1,0:T(8,128)(2,1)S(1)} all-to-all(bf16[8,192,768]{2,1,0:T(8,128)(2,1)S(1)} %get-tuple-element.5), channel_id=1, replica_groups=mesh['rep'=2,'tp'=4,'dp'=4] {'dp'}, dimensions={0} | all-to-all | bytes 4718592 | tf_op jit(solution)/shard_map/all_to_all | solution.py:44
  186.3 1.6 copy.10
  187.8 0.0 all-gather.3.cloned.1.call-update
  187.9 164.3 %all-gather.3.cloned.1.call-done = bf16[2,768,3072]{2,1,0:T(8,128)(2,1)} async-done(((bf16[2,768,768]{2,1,0:T(8,128)(2,1)}), bf16[2,768,3072]{2,1,0:T(8,128)(2,1)}) %all-gather.3.cloned.1.call-update) | async-done | bytes 9437200 | tf_op jit(solution)/shard_map/all_gather | solution.py:45
  352.1 0.0 copy-start
  352.1 6.4 fusion
  358.5 0.0 copy-done
  358.5 9.0 %convolution_convert_fusion.4 = bf16[2,768,768]{2,1,0:T(8,128)(2,1)} fusion(bf16[2,768,3072]{2,1,0:T(8,128)(2,1)S(1)} %copy-done, f32[2]{0:T(128)S(1)} %sqrt_add_fusion), kind=kOutput, calls=%fused_computation.36 | convolution fusion | flops 7263092736 | bytes 11796488 | tf_op jit(solution)/shard_map/bik,bjk->bij/dot_general | solution.py:21
  367.5 20.5 %add_convert_fusion.3 = bf16[2,768,3072]{2,1,0:T(8,128)(2,1)} fusion(bf16[2,768,768]{2,1,0:T(8,128)(2,1)} %convolution_convert_fusion.4, f32[2]{0:T(128)S(1)} %sqrt_add_fusion, bf16[2,768,3072]{2,1,0:T(8,128)(2,1)} %all-gather.3.cloned.1.call-done), kind=kOutput, calls=%fused_computation.7 | convolution fusion | flops 9112780800 | bytes 21233672 | tf_op jit(solution)/shard_map/bij,bjk->bik/dot_general | solution.py:28
  388.1 13.1 %convolution_convert_fusion.3 = bf16[2,768,768]{2,1,0:T(8,128)(2,1)S(1)} fusion(bf16[2,768,3072]{2,1,0:T(8,128)(2,1)} %add_convert_fusion.3), kind=kOutput, calls=%fused_computation.35 | convolution fusion | flops 7248936960 | bytes 11796480 | tf_op jit(solution)/shard_map/bik,bjk->bij/dot_general | solution.py:21
  401.2 18.2 %add_convert_fusion.2 = bf16[2,768,3072]{2,1,0:T(8,128)(2,1)} fusion(bf16[2,768,3072]{2,1,0:T(8,128)(2,1)} %add_convert_fusion.3, bf16[2,768,768]{2,1,0:T(8,128)(2,1)S(1)} %convolution_convert_fusion.3), kind=kOutput, calls=%fused_computation.6 | convolution fusion | flops 9084469248 | bytes 21233664 | tf_op jit(solution)/shard_map/bij,bjk->bik/dot_general | solution.py:28
  419.4 12.8 %convolution_convert_fusion.2 = bf16[2,768,768]{2,1,0:T(8,128)(2,1)S(1)} fusion(bf16[2,768,3072]{2,1,0:T(8,128)(2,1)} %add_convert_fusion.2), kind=kOutput, calls=%fused_computation.34 | convolution fusion | flops 7248936960 | bytes 11796480 | tf_op jit(solution)/shard_map/bik,bjk->bij/dot_general | solution.py:21
  432.3 18.1 %add_convert_fusion.1 = bf16[2,768,3072]{2,1,0:T(8,128)(2,1)} fusion(bf16[2,768,3072]{2,1,0:T(8,128)(2,1)} %add_convert_fusion.2, bf16[2,768,768]{2,1,0:T(8,128)(2,1)S(1)} %convolution_convert_fusion.2), kind=kOutput, calls=%fused_computation.5 | convolution fusion | flops 9084469248 | bytes 21233664 | tf_op jit(solution)/shard_map/bij,bjk->bik/dot_general | solution.py:28
  450.4 13.0 %convolution_convert_fusion.1 = bf16[2,768,768]{2,1,0:T(8,128)(2,1)S(1)} fusion(bf16[2,768,3072]{2,1,0:T(8,128)(2,1)} %add_convert_fusion.1), kind=kOutput, calls=%fused_computation.33 | convolution fusion | flops 7248936960 | bytes 11796480 | tf_op jit(solution)/shard_map/bik,bjk->bij/dot_general | solution.py:21
  463.3 18.2 %add_convert_fusion = bf16[2,768,3072]{2,1,0:T(8,128)(2,1)} fusion(bf16[2,768,3072]{2,1,0:T(8,128)(2,1)} %add_convert_fusion.1, bf16[2,768,768]{2,1,0:T(8,128)(2,1)S(1)} %convolution_convert_fusion.1), kind=kOutput, calls=%fused_computation.4 | convolution fusion | flops 9084469248 | bytes 21233664 | tf_op jit(solution)/shard_map/bij,bjk->bik/dot_general | solution.py:28
  481.6 13.2 %convolution_convert_fusion = bf16[2,768,768]{2,1,0:T(8,128)(2,1)S(1)} fusion(bf16[2,768,3072]{2,1,0:T(8,128)(2,1)} %add_convert_fusion), kind=kOutput, calls=%fused_computation.32 | convolution fusion | flops 7248936960 | bytes 11796480 | tf_op jit(solution)/shard_map/bik,bjk->bij/dot_general | solution.py:21
  494.8 15.5 %fusion.5 = f32[2,768,3072]{2,1,0:T(8,128)} fusion(bf16[2,768,3072]{2,1,0:T(8,128)(2,1)} %add_convert_fusion, bf16[2,768,768]{2,1,0:T(8,128)(2,1)S(1)} %convolution_convert_fusion), kind=kOutput, calls=%fused_computation.21 | convolution fusion | flops 9065594880 | bytes 30670848 | tf_op jit(solution)/shard_map/bij,bjk->bik/dot_general | solution.py:28
  510.3 3.7 fusion.2
  514.0 3.8 copy.11
  517.8 4.6 all-to-all-start.1
  522.4 0.3 all-gather.5.cloned.1.call-start
  523.4 26.4 %all-to-all-done.1 = bf16[2,768,768]{2,0,1:T(2,128)(2,1)S(1)} async-done(((bf16[2,768,768]{2,0,1:T(2,128)(2,1)}), bf16[2,768,768]{2,0,1:T(2,128)(2,1)S(1)}, u32[]{:S(2)}, u32[]{:S(2)}) %all-to-all-start.1) | async-done | bytes 2359328 | tf_op jit(solution)/shard_map/all_to_all | solution.py:51
  549.7 0.0 slice-start
  549.7 2.4 convert_multiply_fusion.1
  552.2 0.0 slice-start.1
  552.2 0.0 copy-start.1
  552.2 0.4 copy.12
  552.7 0.0 slice-done
  552.7 0.6 slice-done.1
  553.2 0.0 copy-done.1
  553.2 4.0 fusion.38
  557.2 0.0 all-gather.5.cloned.1.call-update
  557.2 65.6 %all-gather.5.cloned.1.call-done = bf16[8,768,768]{2,1,0:T(8,128)(2,1)} async-done(((bf16[8,192,768]{2,1,0:T(8,128)(2,1)}), bf16[8,768,768]{2,1,0:T(8,128)(2,1)}) %all-gather.5.cloned.1.call-update) | async-done | bytes 9437200 | tf_op jit(solution)/shard_map/all_gather | solution.py:55
  622.9 8.0 %copy.15 = bf16[8,768,768]{2,1,0:T(8,128)(2,1)} copy(bf16[8,768,768]{2,1,0:T(8,128)(2,1)} %all-gather.5.cloned.1.call-done) | data formatting | bytes 18874368
  (2 shorter events, 0.0 us)
Async XLA Ops:
  7.2 141.3 %reduce-scatter.2.cloned.1.call-start = ((), (), s32[]{:S(2)}) async-start(), calls=%async_computation.3 | async-start | bytes 23592960 | tf_op jit(solution)/shard_map/reduce_scatter | solution.py:40
  7.9 344.2 %all-gather.3.cloned.1.call-start = ((), (), s32[]{:S(2)}) async-start(), calls=%async_computation.4 | async-start | bytes 11796480 | tf_op jit(solution)/shard_map/all_gather | solution.py:45
  352.1 6.4 %copy-start = (bf16[2,768,3072]{2,1,0:T(8,128)(2,1)S(1)}, bf16[2,768,3072]{2,1,0:T(8,128)(2,1)}, u32[]{:S(2)}) copy-start(bf16[2,768,3072]{2,1,0:T(8,128)(2,1)} %all-gather.3.cloned.1.call-done) | copy-start | bytes 28311556
  517.8 31.9 %all-to-all-start.1 = ((bf16[2,768,768]{2,0,1:T(2,128)(2,1)}), bf16[2,768,768]{2,0,1:T(2,128)(2,1)S(1)}, u32[]{:S(2)}, u32[]{:S(2)}) async-start(bf16[2,768,768]{2,0,1:T(2,128)(2,1)} %copy.11), calls=%async_computation.2 | async-start | bytes 4718592 | tf_op jit(solution)/shard_map/all_to_all | solution.py:51
  522.4 100.4 %all-gather.5.cloned.1.call-start = ((), (), s32[]{:S(2)}) async-start(), calls=%async_computation.5 | async-start | bytes 11796480 | tf_op jit(solution)/shard_map/all_gather | solution.py:55
  549.7 2.9 slice-start
  552.2 1.0 slice-start.1
  552.2 1.0 copy-start.1
Sparse Core Ops, SparseCore 0:
  10.6 137.8 reduce-scatter.1
  188.0 164.0 all-gather.2
  557.3 65.4 all-gather.4
where the time goes:
time: 647 us; the launch traced here: 638 us
  waiting for transfers between devices  397 us (61%)
  matrix products  152 us (23%)
  blocking collectives  30.8 us (5%)
  other arithmetic  23.5 us (4%)
  between operations  15 us (2%)
  local copies, waits for them, and re-layouts  14.5 us (2%)
    all_gather x1, waiting for transfers between devices, local_step(): whole_mats = lax.all_gather(whole_rows, 'tp', axis=2, tiled=True)  164 us
    reduce_scatter x1, waiting for transfers between devices, local_step(): lax.psum_scatter(grad_local[0], 'dp', scatter_dimension=1, tiled=True)  141 us
    dot_general x5, matrix products, newton_schulz(): jnp.einsum('bij,bjk->bik', poly_mat, x_cur, preferred_element_type=jnp.fl...  90.7 us
    all_gather x1, waiting for transfers between devices, local_step(): lax.all_gather(weight_new.astype(jnp.bfloat16), 'dp', axis=1, tiled=True)  65.6 us
    dot_general x5, matrix products, newton_schulz(): jnp.einsum('bik,bjk->bij', x_cur, x_cur, preferred_element_type=jnp.float32)  61.1 us
    all_to_all x1, blocking collectives, local_step(): lax.all_to_all(update, 'dp', split_axis=0, concat_axis=1, tiled=True)  30.8 us
    all_to_all x1, waiting for transfers between devices, local_step(): lax.all_to_all(own_cols, 'dp', split_axis=1, concat_axis=0, tiled=True)  26.4 us
  transfers between devices with their start and end apart: 4, of which 4 were waited for; matrix products, arithmetic and copies ran while one was open for 0% of the time, Pallas kernels for 0%

commit v1 on v0

v1 whole, which is shorter than its diff:
```python
import functools
import math
import jax
import jax.numpy as jnp
from jax import lax
from jax.experimental import pallas as pl
from jax.experimental.pallas import tpu as pltpu
from jax.sharding import PartitionSpec as P

MOMENTUM = 0.95
NS_STEPS = 5
COEF_A = 3.4445
COEF_B = -4.7750
COEF_C = 2.0315
NORM_EPS = 1e-7
MESH = pl.DeviceIdType.MESH
F32 = jnp.float32
BF16 = jnp.bfloat16

LAG_IN = 2
LAG_OUT = 2


def owner_of(j):
    half = j // 4
    tp = (j % 2) * (3 - 2 * half) + half
    y = ((j + 1) // 2) % 2
    return tp, y


def matrix_of(tp, y):
    half = ((tp + 1) // 2) % 2
    par = tp // 2
    return 4 * half + par + 2 * ((y + par) % 2)


def kernel(cfg, lr_ref, decay_ref, grad, mom_in, wt_in, mom_o, wt_o, wb_o,
           own, rcv, yr, mom, wt, ub, x, ga, gb, xr, wb, wr,
           s_own, s_mom, s_wt, s_c2s, s_c2r, s_ys, s_yr, s_us, s_ur, s_fs, s_fr, s_xs, s_xr,
           s_mo, s_wo, s_wl, s_ps, s_pr, s_gs, s_gr, s_fl, s_qs, s_qr):
    mats, rows, cols, ncol, out_scale, inv_dp = cfg
    full_rows = 4 * rows
    tp = lax.axis_index("tp")
    dp = lax.axis_index("dp")
    y = dp // 2
    c = dp % 2
    oy = 1 - y
    oc = 1 - c
    dp_core = y * 2 + oc
    dp_y = oy * 2 + c
    mine = matrix_of(tp, y)

    def rowq(q):
        return pl.ds(pl.multiple_of(q * rows, rows), rows)

    def colq(t):
        return pl.ds(pl.multiple_of(t * cols, cols), cols)

    def remote(src, dst, ss, rs, tp_id, dp_id):
        return pltpu.make_async_remote_copy(
            src_ref=src, dst_ref=dst, send_sem=ss, recv_sem=rs,
            device_id={"tp": tp_id, "dp": dp_id}, device_id_type=MESH)

    def own_copy(j, q):
        return pltpu.make_async_copy(grad.at[j, rowq(q * 2 + c), :], own.at[j, q], s_own.at[j, q])

    def mom_copy(j):
        return pltpu.make_async_copy(mom_in.at[j], mom.at[j], s_mom.at[j])

    def wt_copy(j):
        return pltpu.make_async_copy(wt_in.at[j], wt.at[j], s_wt.at[j])

    def core_send(j, q):
        return remote(grad.at[j, rowq(q * 2 + oc), :], rcv.at[j, q], s_c2s.at[j, q], s_c2r.at[j, q], tp, dp_core)

    barrier = pltpu.get_barrier_semaphore()
    pl.semaphore_signal(barrier, inc=1, device_id={"tp": tp, "dp": dp_core}, device_id_type=MESH)
    for k in range(1, 8):
        tgt = (tp * 2 + y + k) % 8
        pl.semaphore_signal(barrier, inc=1, device_id={"tp": tgt // 2, "dp": (tgt % 2) * 2 + c}, device_id_type=MESH)
    for q in range(2):
        own_copy(0, q).start()
    pl.semaphore_wait(barrier, 8)

    @pl.loop(0, mats)
    def _(j):
        for q in range(2):
            core_send(j, q).start()

        @pl.when(j > 0)
        def _():
            for q in range(2):
                own_copy(j, q).start()
        mom_copy(j).start()

    @pl.loop(0, mats)
    def _(j):
        wt_copy(j).start()

    def y_send(j):
        return remote(own.at[j, oy], yr.at[j], s_ys.at[j], s_yr.at[j], tp, dp_y)

    def sum_cores(j):
        for q in range(2):
            own_copy(j, q).wait()
            core_send(j, q).wait_recv()

        @pl.loop(0, rows, step=16)
        def _(r):
            rr = pl.ds(pl.multiple_of(r, 16), 16)
            own[j, oy, rr, :] = own[j, oy, rr, :] + rcv[j, oy, rr, :]
        y_send(j).start()

    def u_send(j, tp_id, dp_id):
        return remote(ub.at[j], x.at[rowq(dp), colq(tp)], s_us.at[j], s_ur.at[y, tp], tp_id, dp_id)

    def sum_y(j):
        y_send(j).wait_recv()
        mom_copy(j).wait()

        @pl.loop(0, rows, step=16)
        def _(r):
            rr = pl.ds(pl.multiple_of(r, 16), 16)
            g = (own[j, y, rr, :] + rcv[j, y, rr, :] + yr[j, rr, :]) * inv_dp
            m = MOMENTUM * mom[j, rr, :] + g
            mom[j, rr, :] = m
            ub[j, rr, :] = (g + MOMENTUM * m).astype(BF16)
        pltpu.make_async_copy(mom.at[j], mom_o.at[j], s_mo.at[j]).start()
        otp, oyy = owner_of(j)

        @pl.when(mine == j)
        def _():
            x[rowq(dp), colq(tp)] = ub[j]

        @pl.when(mine != j)
        def _():
            u_send(j, otp, oyy * 2 + c).start()

    def piece(yy, tt):
        return remote(ub.at[0], x.at[rowq(yy * 2 + c), colq(tt)], s_us.at[0], s_ur.at[yy, tt], tp, dp_core)

    def x_fwd(q):
        blk = x.at[rowq(q * 2 + c), :]
        return remote(blk, blk, s_fs.at[q], s_fr.at[q], tp, dp_core)

    def x_fwd_in(q):
        blk = x.at[rowq(q * 2 + oc), :]
        return remote(blk, blk, s_fs.at[q], s_fr.at[q], tp, dp_core)

    def gather_x():
        for q in range(2):
            for t in range(4):
                @pl.when(jnp.logical_or(y != q, tp != t))
                def _():
                    piece(q, t).wait_recv()
            x_fwd(q).start()
        for q in range(2):
            x_fwd_in(q).wait_recv()
        for q in range(2):
            x_fwd(q).wait_send()

        def body(i, acc):
            rr = pl.ds(pl.multiple_of(i * 16, 16), 16)
            v = x[rr, :].astype(F32)
            v = v * v
            for t in range(ncol // cols):
                acc = acc + v[:, t * cols:(t + 1) * cols]
            return acc
        acc = lax.fori_loop(0, full_rows // 16, body, jnp.zeros((16, cols), F32))
        total = jnp.sum(acc, axis=(0, 1), keepdims=True)
        inv = 1.0 / (jnp.sqrt(total) + NORM_EPS)

        @pl.loop(0, full_rows, step=16)
        def _(r):
            rr = pl.ds(pl.multiple_of(r, 16), 16)
            x[rr, :] = (x[rr, :].astype(F32) * inv).astype(BF16)

    def ns_step():
        blk = min(256, full_rows)

        @pl.loop(0, full_rows, step=blk)
        def _(r):
            rr = pl.ds(pl.multiple_of(r, blk), blk)
            ga[rr, :] = lax.dot_general(x[rr, :], x[...], (((1,), (1,)), ((), ())),
                                        preferred_element_type=F32).astype(BF16)

        @pl.loop(0, full_rows, step=blk)
        def _(r):
            rr = pl.ds(pl.multiple_of(r, blk), blk)
            sq = jnp.dot(ga[rr, :], ga[...], preferred_element_type=F32)
            gb[rr, :] = (COEF_B * ga[rr, :].astype(F32) + COEF_C * sq).astype(BF16)

        cblk = min(512, ncol)

        @pl.loop(0, ncol, step=cblk)
        def _(r):
            rr = pl.ds(pl.multiple_of(r, cblk), cblk)
            prod = jnp.dot(gb[...], x[:, rr], preferred_element_type=F32)
            x[:, rr] = (COEF_A * x[:, rr].astype(F32) + prod).astype(BF16)

    def x_send(q, t):
        return remote(x.at[rowq(q * 2 + c), colq(t)], xr.at[mine], s_xs.at[q, t], s_xr.at[mine], t, q * 2 + c)

    def x_recv(m):
        return remote(x.at[rowq(c), colq(0)], xr.at[m], s_xs.at[0, 0], s_xr.at[m], tp, dp_core)

    def send_back():
        for q in range(2):
            for t in range(4):
                @pl.when(jnp.logical_or(y != q, tp != t))
                def _():
                    x_send(q, t).start()

                @pl.when(jnp.logical_and(y == q, tp == t))
                def _():
                    xr[mine] = x[rowq(q * 2 + c), colq(t)]

    def wb_local(m):
        return pltpu.make_async_copy(wb.at[m], wb_o.at[m, rowq(dp), :], s_wl.at[m])

    def wb_core(m):
        return remote(wb.at[m], wb_o.at[m, rowq(dp), :], s_ps.at[m], s_pr.at[m], tp, dp_core)

    def wb_core_in(m):
        return remote(wb.at[m], wb_o.at[m, rowq(dp_core), :], s_ps.at[m], s_pr.at[m], tp, dp_core)

    def wb_y(m):
        return remote(wb.at[m], wr.at[m], s_gs.at[m], s_gr.at[m], tp, dp_y)

    def update(m):
        @pl.when(mine != m)
        def _():
            x_recv(m).wait_recv()
        wt_copy(m).wait()
        rate = lr_ref[m]
        decay = decay_ref[0]

        @pl.loop(0, rows, step=16)
        def _(r):
            rr = pl.ds(pl.multiple_of(r, 16), 16)
            w = wt[m, rr, :]
            w = w - rate * (out_scale * xr[m, rr, :].astype(F32) + decay * w)
            wt[m, rr, :] = w
            wb[m, rr, :] = w.astype(BF16)
        wb_y(m).start()
        wb_core(m).start()
        wb_local(m).start()
        pltpu.make_async_copy(wt.at[m], wt_o.at[m], s_wo.at[m]).start()

    def fwd_local(m):
        return pltpu.make_async_copy(wr.at[m], wb_o.at[m, rowq(dp_y), :], s_fl.at[m])

    def fwd_core(m):
        return remote(wr.at[m], wb_o.at[m, rowq(dp_y), :], s_qs.at[m], s_qr.at[m], tp, dp_core)

    def fwd_core_in(m):
        return remote(wr.at[m], wb_o.at[m, rowq(oy * 2 + oc), :], s_qs.at[m], s_qr.at[m], tp, dp_core)

    def forward(m):
        wb_y(m).wait_recv()
        fwd_core(m).start()
        fwd_local(m).start()

    first_ns = mine + 1 + LAG_IN
    lag = 1 + LAG_IN + NS_STEPS + LAG_OUT

    @pl.loop(0, mats + lag + 1)
    def _(t):
        @pl.when(t < mats)
        def _():
            sum_cores(t)

        @pl.when(jnp.logical_and(t >= 1, t < mats + 1))
        def _():
            sum_y(t - 1)

        @pl.when(t == first_ns)
        def _():
            gather_x()

        @pl.when(jnp.logical_and(t >= first_ns, t < first_ns + NS_STEPS))
        def _():
            ns_step()

        @pl.when(t == first_ns + NS_STEPS - 1)
        def _():
            send_back()

        @pl.when(jnp.logical_and(t >= lag, t < mats + lag))
        def _():
            update(t - lag)

        @pl.when(t >= lag + 1)
        def _():
            forward(t - lag - 1)

    @pl.loop(0, mats)
    def _(j):
        for q in range(2):
            core_send(j, q).wait_send()
        y_send(j).wait_send()

        @pl.when(mine != j)
        def _():
            u_send(j, tp, dp_core).wait_send()
        pltpu.make_async_copy(mom.at[j], mom_o.at[j], s_mo.at[j]).wait()
        pltpu.make_async_copy(wt.at[j], wt_o.at[j], s_wo.at[j]).wait()
        wb_local(j).wait()
        wb_core(j).wait_send()
        wb_core_in(j).wait_recv()
        wb_y(j).wait_send()
        fwd_local(j).wait()
        fwd_core(j).wait_send()
        fwd_core_in(j).wait_recv()
    for q in range(2):
        for t in range(4):
            @pl.when(jnp.logical_or(y != q, tp != t))
            def _():
                x_send(q, t).wait_send()


def solution(mesh):
    dp_size = mesh.shape["dp"]
    tp_size = mesh.shape["tp"]

    def local_step(grad_local, mom_local, weight_local, learn_rate, decay_rate):
        mats, rows, cols = mom_local.shape
        ncol = cols * tp_size
        nrow = rows * dp_size
        cfg = (mats, rows, cols, ncol, 0.2 * math.sqrt(max(nrow, ncol)), 1.0 / dp_size)
        dma = pltpu.SemaphoreType.DMA
        smem = pl.BlockSpec(memory_space=pltpu.SMEM)
        hbm = pl.BlockSpec(memory_space=pl.ANY)
        return pl.pallas_call(
            functools.partial(kernel, cfg),
            out_shape=(jax.ShapeDtypeStruct((mats, rows, cols), F32),
                       jax.ShapeDtypeStruct((mats, rows, cols), F32),
                       jax.ShapeDtypeStruct((mats, nrow, cols), BF16)),
            in_specs=[smem, smem, hbm, hbm, hbm],
            out_specs=(hbm, hbm, hbm),
            scratch_shapes=[
                pltpu.VMEM((mats, 2, rows, cols), F32),
                pltpu.VMEM((mats, 2, rows, cols), F32),
                pltpu.VMEM((mats, rows, cols), F32),
                pltpu.VMEM((mats, rows, cols), F32),
                pltpu.VMEM((mats, rows, cols), F32),
                pltpu.VMEM((mats, rows, cols), BF16),
                pltpu.VMEM((nrow, ncol), BF16),
                pltpu.VMEM((nrow, nrow), BF16),
                pltpu.VMEM((nrow, nrow), BF16),
                pltpu.VMEM((mats, rows, cols), BF16),
                pltpu.VMEM((mats, rows, cols), BF16),
                pltpu.VMEM((mats, rows, cols), BF16),
                dma((mats, 2)), dma((mats,)), dma((mats,)),
                dma((mats, 2)), dma((mats, 2)),
                dma((mats,)), dma((mats,)),
                dma((mats,)), dma((2, tp_size)),
                dma((2,)), dma((2,)),
                dma((2, tp_size)), dma((mats,)),
                dma((mats,)), dma((mats,)), dma((mats,)),
                dma((mats,)), dma((mats,)), dma((mats,)), dma((mats,)),
                dma((mats,)), dma((mats,)), dma((mats,)),
            ],
            compiler_params=pltpu.CompilerParams(
                collective_id=0, has_side_effects=True, vmem_limit_bytes=66 * 1024 * 1024 - 2 ** 21),
            name="muon_step",
        )(learn_rate, decay_rate.reshape(1), grad_local[0], mom_local, weight_local)

    return jax.shard_map(
        local_step,
        mesh=mesh,
        in_specs=(P(("rep", "dp"), None, None, "tp"), P("rep", "dp", "tp"), P("rep", "dp", "tp"), P("rep"), P()),
        out_specs=(P("rep", "dp", "tp"), P("rep", "dp", "tp"), P("rep", None, "tp")),
        check_vma=False,
    )
```

time: 647 us -> 316 us (0.49); the launches traced: 638 us -> 315 us
  waiting for transfers between devices: 397 us -> 0 us
  Pallas kernels: 0 us -> 299 us
  matrix products: 152 us -> 0 us
  blocking collectives: 30.8 us -> 0 us
  other arithmetic: 23.5 us -> 0 us
  between operations: 15 us -> 1.3 us
    pallas_call x0 -> x1, Pallas kernels: none -> 299 us  [local_step(): pl.pallas_call(functools.partial(kernel, cfg), out_shape=(jax.ShapeDtypeS...]
    all_gather x2 -> x0, waiting for transfers between devices: 230 us -> none  [the longest x1 164 us: local_step(): whole_mats = lax.all_gather(whole_rows, 'tp', axis=2, tiled=True)]
    dot_general x10 -> x0, matrix products: 152 us -> none  [the longest x5 90.7 us: newton_schulz(): jnp.einsum('bij,bjk->bik', poly_mat, x_cur, preferred_element_type=jnp.fl...]
    reduce_scatter x1 -> x0, waiting for transfers between devices: 141 us -> none  [local_step(): lax.psum_scatter(grad_local[0], 'dp', scatter_dimension=1, tiled=True)]
    all_to_all x1 -> x0, blocking collectives: 30.8 us -> none  [local_step(): lax.all_to_all(update, 'dp', split_axis=0, concat_axis=1, tiled=True)]
    all_to_all x1 -> x0, waiting for transfers between devices: 26.4 us -> none  [local_step(): lax.all_to_all(own_cols, 'dp', split_axis=1, concat_axis=0, tiled=True)]
    convert_element_type x3 -> x0, other arithmetic: 14.7 us -> none  [the longest x1 6.99 us: local_step(): update = (grad_mean + MOMENTUM * mom_new).astype(jnp.bfloat16)]
    unnamed x9 -> x5, local copies, waits for them, and re-layouts: 8.61 us -> 15.2 us
  transfers between devices with their start and end apart: 4 -> 0, of which waited for: 4 -> 0; matrix products, arithmetic and copies ran while one was open for 0% -> 0% of each run, Pallas kernels for 0% -> 0%
where the time goes in v1:
time: 316 us; the launch traced here: 315 us
  Pallas kernels  299 us (95%)
  local copies, waits for them, and re-layouts  15.2 us (5%)
    pallas_call x1, Pallas kernels, local_step(): pl.pallas_call(functools.partial(kernel, cfg), out_shape=(jax.ShapeDtypeS...  299 us
    unnamed x5, local copies, waits for them, and re-layouts  15.2 us

profile of v1, /device:TPU:11, one launch (start us, length us, event | category | flops | bytes accessed | tf_op | source)
XLA Modules:
  0.0 315.5 jit_solution(11726596994294944065)
XLA Ops:
  1.3 299.0 %muon_step.1 = (f32[8,192,768]{2,1,0:T(8,128)}, f32[8,192,768]{2,1,0:T(8,128)}, bf16[8,768,768]{2,1,0:T(8,128)(2,1)}) custom-call(f32[8]{0:T(128)} %lr_ref.1, f32[1]{0:T(128)} %bitcast.2.decay_ref, f32[8,768,768]{2,1,0:T(8,128)} %bitcast.3, f32[8,192,768]{2,1,0:T(8,128)} %mom_in.1, f32[8,192,768]{2,1,0:T(8,128)} %wt_in.1), custom_call_target="tpu_custom_call" | custom-call | tf_op jit(solution)/shard_map/muon_step/pallas_call | solution.py:334
  300.3 0.0 copy-start
  300.3 5.0 %copy.12 = f32[8,192,768]{2,1,0:T(8,128)} copy(f32[8,192,768]{2,1,0:T(8,128)} %get-tuple-element.6) | data formatting | bytes 9437184
  305.3 0.0 copy-done
  305.3 2.2 copy.13
  307.4 8.0 %copy.14 = bf16[8,768,768]{2,1,0:T(8,128)(2,1)} copy(bf16[8,768,768]{2,1,0:T(8,128)(2,1)} %get-tuple-element.8) | data formatting | bytes 18874368
Async XLA Ops:
  300.3 5.0 %copy-start = (f32[8,192,768]{2,1,0:T(8,128)S(1)}, f32[8,192,768]{2,1,0:T(8,128)}, u32[]{:S(2)}) copy-start(f32[8,192,768]{2,1,0:T(8,128)} %get-tuple-element.7) | copy-start | bytes 14155780

commit v2 on v1

--- a/solution.py
+++ b/solution.py
@@ -17,8 +17,12 @@
 F32 = jnp.float32
 BF16 = jnp.bfloat16
 
-LAG_IN = 2
-LAG_OUT = 2
+LAG_IN = 3
+LAG_UPD = 13
+LAG_FWD = 3
+HELD, GUARD = 1, 6
+FAST_SLOTS = 6
+AHEAD = 2
 
 
 def owner_of(j):
@@ -35,9 +39,9 @@
 
 
 def kernel(cfg, lr_ref, decay_ref, grad, mom_in, wt_in, mom_o, wt_o, wb_o,
-           own, rcv, yr, mom, wt, ub, x, ga, gb, xr, wb, wr,
+           own, rcv, yr, mom, wt, ub, x, ga, gb, uf, acc, xr, wb, wr,
            s_own, s_mom, s_wt, s_c2s, s_c2r, s_ys, s_yr, s_us, s_ur, s_fs, s_fr, s_xs, s_xr,
-           s_mo, s_wo, s_wl, s_ps, s_pr, s_gs, s_gr, s_fl, s_qs, s_qr):
+           s_hs, s_hr, s_vs, s_mo, s_wo, s_wl, s_ps, s_pr, s_gs, s_gr, s_fl, s_qs, s_qr, s_go):
     mats, rows, cols, ncol, out_scale, inv_dp = cfg
     full_rows = 4 * rows
     tp = lax.axis_index("tp")
@@ -78,32 +82,26 @@
     for k in range(1, 8):
         tgt = (tp * 2 + y + k) % 8
         pl.semaphore_signal(barrier, inc=1, device_id={"tp": tgt // 2, "dp": (tgt % 2) * 2 + c}, device_id_type=MESH)
-    for q in range(2):
-        own_copy(0, q).start()
+    own_copy(0, oy).start()
     pl.semaphore_wait(barrier, 8)
 
-    @pl.loop(0, mats)
-    def _(j):
-        for q in range(2):
-            core_send(j, q).start()
-
-        @pl.when(j > 0)
-        def _():
-            for q in range(2):
-                own_copy(j, q).start()
+    def issue(j, first):
+        core_send(j, oy).start()
+        if not first:
+            own_copy(j, oy).start()
+        core_send(j, y).start()
+        own_copy(j, y).start()
         mom_copy(j).start()
 
-    @pl.loop(0, mats)
-    def _(j):
-        wt_copy(j).start()
+    for j in range(AHEAD):
+        issue(j, j == 0)
 
     def y_send(j):
         return remote(own.at[j, oy], yr.at[j], s_ys.at[j], s_yr.at[j], tp, dp_y)
 
     def sum_cores(j):
-        for q in range(2):
-            own_copy(j, q).wait()
-            core_send(j, q).wait_recv()
+        own_copy(j, oy).wait()
+        core_send(j, oy).wait_recv()
 
         @pl.loop(0, rows, step=16)
         def _(r):
@@ -115,8 +113,10 @@
         return remote(ub.at[j], x.at[rowq(dp), colq(tp)], s_us.at[j], s_ur.at[y, tp], tp_id, dp_id)
 
     def sum_y(j):
+        own_copy(j, y).wait()
+        core_send(j, y).wait_recv()
+        mom_copy(j).wait()
         y_send(j).wait_recv()
-        mom_copy(j).wait()
 
         @pl.loop(0, rows, step=16)
         def _(r):
@@ -126,48 +126,77 @@
             mom[j, rr, :] = m
             ub[j, rr, :] = (g + MOMENTUM * m).astype(BF16)
         pltpu.make_async_copy(mom.at[j], mom_o.at[j], s_mo.at[j]).start()
+        wt_copy(j).start()
         otp, oyy = owner_of(j)
 
         @pl.when(mine == j)
         def _():
             x[rowq(dp), colq(tp)] = ub[j]
 
-        @pl.when(mine != j)
-        def _():
-            u_send(j, otp, oyy * 2 + c).start()
+        @pl.when(jnp.logical_and(mine != j, y == oyy))
+        def _():
+            u_send(j, otp, dp).start()
+
+        @pl.when(y != oyy)
+        def _():
+            u_cross(j).start()
+
+    def u_cross(j):
+        return remote(ub.at[j], uf.at[j], s_hs.at[j], s_hr.at[j], tp, dp_y)
+
+    def u_pass(j, tp_id, dp_id):
+        return remote(uf.at[j], x.at[rowq(dp_y), colq(tp)], s_vs.at[j], s_ur.at[oy, tp], tp_id, dp_id)
+
+    def hop(j):
+        otp, oyy = owner_of(j)
+
+        @pl.when(y == oyy)
+        def _():
+            u_cross(j).wait_recv()
+
+            @pl.when(mine == j)
+            def _():
+                x[rowq(dp_y), colq(tp)] = uf[j]
+
+            @pl.when(mine != j)
+            def _():
+                u_pass(j, otp, dp).start()
 
     def piece(yy, tt):
         return remote(ub.at[0], x.at[rowq(yy * 2 + c), colq(tt)], s_us.at[0], s_ur.at[yy, tt], tp, dp_core)
 
-    def x_fwd(q):
-        blk = x.at[rowq(q * 2 + c), :]
-        return remote(blk, blk, s_fs.at[q], s_fr.at[q], tp, dp_core)
-
-    def x_fwd_in(q):
-        blk = x.at[rowq(q * 2 + oc), :]
-        return remote(blk, blk, s_fs.at[q], s_fr.at[q], tp, dp_core)
+    def x_fwd(q, t):
+        blk = x.at[rowq(q * 2 + c), colq(t)]
+        return remote(blk, blk, s_fs.at[q, t], s_fr.at[q, t], tp, dp_core)
+
+    def x_fwd_in(q, t):
+        blk = x.at[rowq(q * 2 + oc), colq(t)]
+        return remote(blk, blk, s_fs.at[q, t], s_fr.at[q, t], tp, dp_core)
+
+    def add_squares(q, t):
+        def body(i, carry):
+            v = x[pl.ds(pl.multiple_of(q * rows + i * 16, 16), 16), colq(t)].astype(F32)
+            return carry + v * v
+        acc[...] = lax.fori_loop(0, rows // 16, body, acc[...])
 
     def gather_x():
+        acc[...] = jnp.zeros_like(acc)
+        for q in (y, oy):
+            for k in range(4):
+                t = (tp + k) % 4
+                if k > 0:
+                    piece(q, t).wait_recv()
+                x_fwd(q, t).start()
+                add_squares(q * 2 + c, t)
+        for q in (y, oy):
+            for k in range(4):
+                t = (tp + k) % 4
+                x_fwd_in(q, t).wait_recv()
+                add_squares(q * 2 + oc, t)
         for q in range(2):
             for t in range(4):
-                @pl.when(jnp.logical_or(y != q, tp != t))
-                def _():
-                    piece(q, t).wait_recv()
-            x_fwd(q).start()
-        for q in range(2):
-            x_fwd_in(q).wait_recv()
-        for q in range(2):
-            x_fwd(q).wait_send()
-
-        def body(i, acc):
-            rr = pl.ds(pl.multiple_of(i * 16, 16), 16)
-            v = x[rr, :].astype(F32)
-            v = v * v
-            for t in range(ncol // cols):
-                acc = acc + v[:, t * cols:(t + 1) * cols]
-            return acc
-        acc = lax.fori_loop(0, full_rows // 16, body, jnp.zeros((16, cols), F32))
-        total = jnp.sum(acc, axis=(0, 1), keepdims=True)
+                x_fwd(q, t).wait_send()
+        total = jnp.sum(acc[...], axis=(0, 1), keepdims=True)
         inv = 1.0 / (jnp.sqrt(total) + NORM_EPS)
 
         @pl.loop(0, full_rows, step=16)
@@ -175,22 +204,30 @@
             rr = pl.ds(pl.multiple_of(r, 16), 16)
             x[rr, :] = (x[rr, :].astype(F32) * inv).astype(BF16)
 
+    blk = min(256, full_rows // 2)
+    strips = full_rows // blk
+
+    def mirror(dst, i, strip):
+        for k in range(i + 1, strips):
+            dst[k * blk:(k + 1) * blk, i * blk:(i + 1) * blk] = strip[:, (k - i) * blk:(k - i + 1) * blk].T
+
+    def gram():
+        for i in range(strips):
+            lo = i * blk
+            strip = lax.dot_general(x[lo:lo + blk, :], x[lo:, :], (((1,), (1,)), ((), ())),
+                                    preferred_element_type=F32).astype(BF16)
+            ga[lo:lo + blk, lo:] = strip
+            mirror(ga, i, strip)
+
     def ns_step():
-        blk = min(256, full_rows)
-
-        @pl.loop(0, full_rows, step=blk)
-        def _(r):
-            rr = pl.ds(pl.multiple_of(r, blk), blk)
-            ga[rr, :] = lax.dot_general(x[rr, :], x[...], (((1,), (1,)), ((), ())),
-                                        preferred_element_type=F32).astype(BF16)
-
-        @pl.loop(0, full_rows, step=blk)
-        def _(r):
-            rr = pl.ds(pl.multiple_of(r, blk), blk)
-            sq = jnp.dot(ga[rr, :], ga[...], preferred_element_type=F32)
-            gb[rr, :] = (COEF_B * ga[rr, :].astype(F32) + COEF_C * sq).astype(BF16)
-
-        cblk = min(512, ncol)
+        gram()
+        for i in range(strips):
+            lo = i * blk
+            sq = jnp.dot(ga[lo:lo + blk, :], ga[:, lo:], preferred_element_type=F32)
+            strip = (COEF_B * ga[lo:lo + blk, lo:].astype(F32) + COEF_C * sq).astype(BF16)
+            gb[lo:lo + blk, lo:] = strip
+            mirror(gb, i, strip)
+        cblk = ncol // 2
 
         @pl.loop(0, ncol, step=cblk)
         def _(r):
@@ -198,22 +235,40 @@
             prod = jnp.dot(gb[...], x[:, rr], preferred_element_type=F32)
             x[:, rr] = (COEF_A * x[:, rr].astype(F32) + prod).astype(BF16)
 
+    def ns_last():
+        gram()
+        for q in range(2):
+            part = ga[rowq(q * 2 + c), :]
+            sq = jnp.dot(part, ga[...], preferred_element_type=F32)
+            gb[q * rows:(q + 1) * rows, :] = (COEF_B * part.astype(F32) + COEF_C * sq).astype(BF16)
+
+        @pl.loop(0, 4)
+        def _(i):
+            t = i + (3 - 2 * i) * (1 - tp // 2)
+            prod = jnp.dot(gb[:2 * rows, :], x[:, colq(t)], preferred_element_type=F32)
+            for q in range(2):
+                rr = rowq(q * 2 + c)
+                x[rr, colq(t)] = (COEF_A * x[rr, colq(t)].astype(F32)
+                                  + prod[q * rows:(q + 1) * rows, :]).astype(BF16)
+            @pl.when(mine != HELD)
+            def _():
+                for q in range(2):
+                    send_back(q, t)
+
     def x_send(q, t):
         return remote(x.at[rowq(q * 2 + c), colq(t)], xr.at[mine], s_xs.at[q, t], s_xr.at[mine], t, q * 2 + c)
 
     def x_recv(m):
         return remote(x.at[rowq(c), colq(0)], xr.at[m], s_xs.at[0, 0], s_xr.at[m], tp, dp_core)
 
-    def send_back():
-        for q in range(2):
-            for t in range(4):
-                @pl.when(jnp.logical_or(y != q, tp != t))
-                def _():
-                    x_send(q, t).start()
-
-                @pl.when(jnp.logical_and(y == q, tp == t))
-                def _():
-                    xr[mine] = x[rowq(q * 2 + c), colq(t)]
+    def send_back(q, t):
+        @pl.when(jnp.logical_or(y != q, tp != t))
+        def _():
+            x_send(q, t).start()
+
+        @pl.when(jnp.logical_and(y == q, tp == t))
+        def _():
+            xr[mine] = x[rowq(q * 2 + c), colq(t)]
 
     def wb_local(m):
         return pltpu.make_async_copy(wb.at[m], wb_o.at[m, rowq(dp), :], s_wl.at[m])
@@ -262,37 +317,69 @@
         fwd_local(m).start()
 
     first_ns = mine + 1 + LAG_IN
-    lag = 1 + LAG_IN + NS_STEPS + LAG_OUT
-
-    @pl.loop(0, mats + lag + 1)
+
+    def steps_before(t):
+        done = t - first_ns + jnp.maximum(jnp.minimum(t, FAST_SLOTS) - first_ns, 0)
+        return jnp.minimum(jnp.maximum(done, 0), NS_STEPS)
+
+
+    sum_cores(0)
+
+    @pl.loop(0, mats + LAG_UPD + LAG_FWD)
     def _(t):
-        @pl.when(t < mats)
-        def _():
-            sum_cores(t)
+        @pl.when(t < mats - AHEAD)
+        def _():
+            issue(t + AHEAD, False)
 
         @pl.when(jnp.logical_and(t >= 1, t < mats + 1))
         def _():
             sum_y(t - 1)
 
+        @pl.when(t < mats - 1)
+        def _():
+            sum_cores(t + 1)
+
+        @pl.when(jnp.logical_and(t >= 2, t < mats + 2))
+        def _():
+            hop(t - 2)
+
+        @pl.when(jnp.logical_and(t == mats + 2, mine == HELD))
+        def _():
+            pl.semaphore_wait(s_go, 1)
+
+            @pl.loop(0, 4)
+            def _(i):
+                k = i + (3 - 2 * i) * (1 - tp // 2)
+                for q in range(2):
+                    send_back(q, k)
+
+        @pl.when(jnp.logical_and(t >= LAG_UPD, t < mats + LAG_UPD))
+        def _():
+            update(t - LAG_UPD)
+
+        @pl.when(t >= LAG_UPD + LAG_FWD)
+        def _():
+            forward(t - LAG_UPD - LAG_FWD)
+
         @pl.when(t == first_ns)
         def _():
             gather_x()
 
-        @pl.when(jnp.logical_and(t >= first_ns, t < first_ns + NS_STEPS))
-        def _():
+            @pl.when(mine == GUARD)
+            def _():
+                htp, hy = owner_of(HELD)
+                pl.semaphore_signal(s_go, inc=1, device_id={"tp": htp, "dp": hy * 2 + c}, device_id_type=MESH)
+
+        begin = steps_before(t)
+        end = steps_before(t + 1)
+
+        @pl.loop(begin, jnp.minimum(end, NS_STEPS - 1))
+        def _(i):
             ns_step()
 
-        @pl.when(t == first_ns + NS_STEPS - 1)
-        def _():
-            send_back()
-
-        @pl.when(jnp.logical_and(t >= lag, t < mats + lag))
-        def _():
-            update(t - lag)
-
-        @pl.when(t >= lag + 1)
-        def _():
-            forward(t - lag - 1)
+        @pl.when(jnp.logical_and(begin < NS_STEPS, end == NS_STEPS))
+        def _():
+            ns_last()
 
     @pl.loop(0, mats)
     def _(j):
@@ -300,9 +387,16 @@
             core_send(j, q).wait_send()
         y_send(j).wait_send()
 
-        @pl.when(mine != j)
+        otp, oyy = owner_of(j)
+
+        @pl.when(jnp.logical_and(mine != j, y == oyy))
         def _():
             u_send(j, tp, dp_core).wait_send()
+            u_pass(j, tp, dp_core).wait_send()
+
+        @pl.when(y != oyy)
+        def _():
+            u_cross(j).wait_send()
         pltpu.make_async_copy(mom.at[j], mom_o.at[j], s_mo.at[j]).wait()
         pltpu.make_async_copy(wt.at[j], wt_o.at[j], s_wo.at[j]).wait()
         wb_local(j).wait()
@@ -349,17 +443,21 @@
                 pltpu.VMEM((nrow, nrow), BF16),
                 pltpu.VMEM((nrow, nrow), BF16),
                 pltpu.VMEM((mats, rows, cols), BF16),
+                pltpu.VMEM((16, cols), F32),
+                pltpu.VMEM((mats, rows, cols), BF16),
                 pltpu.VMEM((mats, rows, cols), BF16),
                 pltpu.VMEM((mats, rows, cols), BF16),
                 dma((mats, 2)), dma((mats,)), dma((mats,)),
                 dma((mats, 2)), dma((mats, 2)),
                 dma((mats,)), dma((mats,)),
                 dma((mats,)), dma((2, tp_size)),
-                dma((2,)), dma((2,)),
+                dma((2, tp_size)), dma((2, tp_size)),
                 dma((2, tp_size)), dma((mats,)),
+                dma((mats,)), dma((mats,)), dma((mats,)),
                 dma((mats,)), dma((mats,)), dma((mats,)),
                 dma((mats,)), dma((mats,)), dma((mats,)), dma((mats,)),
                 dma((mats,)), dma((mats,)), dma((mats,)),
+                pltpu.SemaphoreType.REGULAR,
             ],
             compiler_params=pltpu.CompilerParams(
                 collective_id=0, has_side_effects=True, vmem_limit_bytes=66 * 1024 * 1024 - 2 ** 21),

time: 316 us -> 273 us (0.86)
  Pallas kernels: 299 us -> 256 us
    pallas_call x1, Pallas kernels: 299 us -> 256 us  [local_step(): pl.pallas_call(functools.partial(kernel, cfg), out_shape=(jax.ShapeDtypeS...]
where the time goes in v2:
time: 273 us
  Pallas kernels  256 us (94%)
  local copies, waits for them, and re-layouts  15.2 us (6%)
    pallas_call x1, Pallas kernels, local_step(): pl.pallas_call(functools.partial(kernel, cfg), out_shape=(jax.ShapeDtypeS...  256 us
    unnamed x5, local copies, waits for them, and re-layouts  15.2 us

profile of v2, /device:TPU:11, one launch (start us, length us, event | category | flops | bytes accessed | tf_op | source)
XLA Modules:
  0.0 272.6 jit_solution(11262448235413227255)
XLA Ops:
  1.3 256.1 %muon_step.1 = (f32[8,192,768]{2,1,0:T(8,128)}, f32[8,192,768]{2,1,0:T(8,128)}, bf16[8,768,768]{2,1,0:T(8,128)(2,1)}) custom-call(f32[8]{0:T(128)} %lr_ref.1, f32[1]{0:T(128)} %bitcast.2.decay_ref, f32[8,768,768]{2,1,0:T(8,128)} %bitcast.3, f32[8,192,768]{2,1,0:T(8,128)} %mom_in.1, f32[8,192,768]{2,1,0:T(8,128)} %wt_in.1), custom_call_target="tpu_custom_call" | custom-call | tf_op jit(solution)/shard_map/muon_step/pallas_call | solution.py:428
  257.4 0.0 copy-start
  257.4 5.0 %copy.12 = f32[8,192,768]{2,1,0:T(8,128)} copy(f32[8,192,768]{2,1,0:T(8,128)} %get-tuple-element.6) | data formatting | bytes 9437184
  262.4 0.0 copy-done
  262.4 2.2 copy.13
  264.6 8.0 %copy.14 = bf16[8,768,768]{2,1,0:T(8,128)(2,1)} copy(bf16[8,768,768]{2,1,0:T(8,128)(2,1)} %get-tuple-element.8) | data formatting | bytes 18874368
Async XLA Ops:
  257.4 5.0 %copy-start = (f32[8,192,768]{2,1,0:T(8,128)S(1)}, f32[8,192,768]{2,1,0:T(8,128)}, u32[]{:S(2)}) copy-start(f32[8,192,768]{2,1,0:T(8,128)} %get-tuple-element.7) | copy-start | bytes 14155780

commit v3 on v2

--- a/solution.py
+++ b/solution.py
@@ -17,31 +17,36 @@
 F32 = jnp.float32
 BF16 = jnp.bfloat16
 
-LAG_IN = 3
-LAG_UPD = 13
+OWNERS = ((2, 0), (1, 1), (3, 1), (0, 0), (0, 1), (3, 0), (1, 0), (2, 1))
+DIRECT = ()
+CROSS_SLOT = 9
+AHEAD = 2
+VMEM_MIB = 44
+FAST_SLOTS = (6, 9)
+EARLY = 10
+LATE = 13
 LAG_FWD = 3
-HELD, GUARD = 1, 6
-FAST_SLOTS = 6
-AHEAD = 2
 
 
 def owner_of(j):
-    half = j // 4
-    tp = (j % 2) * (3 - 2 * half) + half
-    y = ((j + 1) // 2) % 2
+    tp, y = 0, 0
+    for k, (tp_k, y_k) in enumerate(OWNERS):
+        tp = tp + jnp.where(j == k, tp_k, 0)
+        y = y + jnp.where(j == k, y_k, 0)
     return tp, y
 
 
 def matrix_of(tp, y):
-    half = ((tp + 1) // 2) % 2
-    par = tp // 2
-    return 4 * half + par + 2 * ((y + par) % 2)
-
-
-def kernel(cfg, lr_ref, decay_ref, grad, mom_in, wt_in, mom_o, wt_o, wb_o,
-           own, rcv, yr, mom, wt, ub, x, ga, gb, uf, acc, xr, wb, wr,
+    mine = 0
+    for k, (tp_k, y_k) in enumerate(OWNERS):
+        mine = mine + jnp.where(jnp.logical_and(tp == tp_k, y == y_k), k, 0)
+    return mine
+
+
+def kernel(cfg, lr_ref, decay_ref, grad, mom_in, wt_in, mom, wt, wb,
+           own, rcv, yr, ub, x, ga, gb, uf, acc, xr,
            s_own, s_mom, s_wt, s_c2s, s_c2r, s_ys, s_yr, s_us, s_ur, s_fs, s_fr, s_xs, s_xr,
-           s_hs, s_hr, s_vs, s_mo, s_wo, s_wl, s_ps, s_pr, s_gs, s_gr, s_fl, s_qs, s_qr, s_go):
+           s_hs, s_hr, s_vs, s_ps, s_pr, s_gs, s_gr, s_qs, s_qr):
     mats, rows, cols, ncol, out_scale, inv_dp = cfg
     full_rows = 4 * rows
     tp = lax.axis_index("tp")
@@ -109,6 +114,12 @@
             own[j, oy, rr, :] = own[j, oy, rr, :] + rcv[j, oy, rr, :]
         y_send(j).start()
 
+    def is_direct(j):
+        hit = 0
+        for k, tp_k, c_k in DIRECT:
+            hit = hit + jnp.where(jnp.logical_and(j == k, jnp.logical_and(tp == tp_k, c == c_k)), 1, 0)
+        return hit
+
     def u_send(j, tp_id, dp_id):
         return remote(ub.at[j], x.at[rowq(dp), colq(tp)], s_us.at[j], s_ur.at[y, tp], tp_id, dp_id)
 
@@ -125,7 +136,6 @@
             m = MOMENTUM * mom[j, rr, :] + g
             mom[j, rr, :] = m
             ub[j, rr, :] = (g + MOMENTUM * m).astype(BF16)
-        pltpu.make_async_copy(mom.at[j], mom_o.at[j], s_mo.at[j]).start()
         wt_copy(j).start()
         otp, oyy = owner_of(j)
 
@@ -137,7 +147,13 @@
         def _():
             u_send(j, otp, dp).start()
 
-        @pl.when(y != oyy)
+        direct = is_direct(j)
+
+        @pl.when(jnp.logical_and(y != oyy, direct == 1))
+        def _():
+            u_send(j, otp, oyy * 2 + c).start()
+
+        @pl.when(jnp.logical_and(y != oyy, direct == 0))
         def _():
             u_cross(j).start()
 
@@ -150,7 +166,7 @@
     def hop(j):
         otp, oyy = owner_of(j)
 
-        @pl.when(y == oyy)
+        @pl.when(jnp.logical_and(y == oyy, is_direct(j) == 0))
         def _():
             u_cross(j).wait_recv()
 
@@ -219,7 +235,7 @@
             ga[lo:lo + blk, lo:] = strip
             mirror(ga, i, strip)
 
-    def ns_step():
+    def ns_poly():
         gram()
         for i in range(strips):
             lo = i * blk
@@ -227,6 +243,8 @@
             strip = (COEF_B * ga[lo:lo + blk, lo:].astype(F32) + COEF_C * sq).astype(BF16)
             gb[lo:lo + blk, lo:] = strip
             mirror(gb, i, strip)
+
+    def ns_apply():
         cblk = ncol // 2
 
         @pl.loop(0, ncol, step=cblk)
@@ -250,10 +268,11 @@
                 rr = rowq(q * 2 + c)
                 x[rr, colq(t)] = (COEF_A * x[rr, colq(t)].astype(F32)
                                   + prod[q * rows:(q + 1) * rows, :]).astype(BF16)
-            @pl.when(mine != HELD)
-            def _():
-                for q in range(2):
-                    send_back(q, t)
+            send_back(y, t)
+
+        @pl.when(mine >= 2)
+        def _():
+            send_cross()
 
     def x_send(q, t):
         return remote(x.at[rowq(q * 2 + c), colq(t)], xr.at[mine], s_xs.at[q, t], s_xr.at[mine], t, q * 2 + c)
@@ -270,17 +289,32 @@
         def _():
             xr[mine] = x[rowq(q * 2 + c), colq(t)]
 
-    def wb_local(m):
-        return pltpu.make_async_copy(wb.at[m], wb_o.at[m, rowq(dp), :], s_wl.at[m])
+    def send_cross():
+        @pl.loop(0, 4)
+        def _(i):
+            send_back(oy, i + (3 - 2 * i) * (1 - tp // 2))
+
+    def wb_send(m, ss, rs, rows_id, dp_id):
+        part = wb.at[m, rowq(rows_id), :]
+        return remote(part, part, ss.at[m], rs.at[m], tp, dp_id)
 
     def wb_core(m):
-        return remote(wb.at[m], wb_o.at[m, rowq(dp), :], s_ps.at[m], s_pr.at[m], tp, dp_core)
+        return wb_send(m, s_ps, s_pr, dp, dp_core)
 
     def wb_core_in(m):
-        return remote(wb.at[m], wb_o.at[m, rowq(dp_core), :], s_ps.at[m], s_pr.at[m], tp, dp_core)
+        return wb_send(m, s_ps, s_pr, dp_core, dp_core)
 
     def wb_y(m):
-        return remote(wb.at[m], wr.at[m], s_gs.at[m], s_gr.at[m], tp, dp_y)
+        return wb_send(m, s_gs, s_gr, dp, dp_y)
+
+    def wb_y_in(m):
+        return wb_send(m, s_gs, s_gr, dp_y, dp_y)
+
+    def fwd_core(m):
+        return wb_send(m, s_qs, s_qr, dp_y, dp_core)
+
+    def fwd_core_in(m):
+        return wb_send(m, s_qs, s_qr, oy * 2 + oc, dp_core)
 
     def update(m):
         @pl.when(mine != m)
@@ -296,36 +330,25 @@
             w = wt[m, rr, :]
             w = w - rate * (out_scale * xr[m, rr, :].astype(F32) + decay * w)
             wt[m, rr, :] = w
-            wb[m, rr, :] = w.astype(BF16)
+            wb[m, pl.ds(pl.multiple_of(dp * rows + r, 16), 16), :] = w.astype(BF16)
         wb_y(m).start()
         wb_core(m).start()
-        wb_local(m).start()
-        pltpu.make_async_copy(wt.at[m], wt_o.at[m], s_wo.at[m]).start()
-
-    def fwd_local(m):
-        return pltpu.make_async_copy(wr.at[m], wb_o.at[m, rowq(dp_y), :], s_fl.at[m])
-
-    def fwd_core(m):
-        return remote(wr.at[m], wb_o.at[m, rowq(dp_y), :], s_qs.at[m], s_qr.at[m], tp, dp_core)
-
-    def fwd_core_in(m):
-        return remote(wr.at[m], wb_o.at[m, rowq(oy * 2 + oc), :], s_qs.at[m], s_qr.at[m], tp, dp_core)
 
     def forward(m):
-        wb_y(m).wait_recv()
+        wb_y_in(m).wait_recv()
         fwd_core(m).start()
-        fwd_local(m).start()
-
-    first_ns = mine + 1 + LAG_IN
-
-    def steps_before(t):
-        done = t - first_ns + jnp.maximum(jnp.minimum(t, FAST_SLOTS) - first_ns, 0)
-        return jnp.minimum(jnp.maximum(done, 0), NS_STEPS)
-
+
+    first_ns = mine + 4 - jnp.where(mine < 2, 1, 0)
+
+    def halves_before(t):
+        done = 2 * (t - first_ns)
+        for until in FAST_SLOTS:
+            done = done + jnp.maximum(jnp.minimum(t, until) - first_ns, 0)
+        return jnp.minimum(jnp.maximum(done, 0), 2 * NS_STEPS)
 
     sum_cores(0)
 
-    @pl.loop(0, mats + LAG_UPD + LAG_FWD)
+    @pl.loop(0, mats + LATE + LAG_FWD)
     def _(t):
         @pl.when(t < mats - AHEAD)
         def _():
@@ -343,41 +366,48 @@
         def _():
             hop(t - 2)
 
-        @pl.when(jnp.logical_and(t == mats + 2, mine == HELD))
-        def _():
-            pl.semaphore_wait(s_go, 1)
-
-            @pl.loop(0, 4)
-            def _(i):
-                k = i + (3 - 2 * i) * (1 - tp // 2)
-                for q in range(2):
-                    send_back(q, k)
-
-        @pl.when(jnp.logical_and(t >= LAG_UPD, t < mats + LAG_UPD))
-        def _():
-            update(t - LAG_UPD)
-
-        @pl.when(t >= LAG_UPD + LAG_FWD)
-        def _():
-            forward(t - LAG_UPD - LAG_FWD)
+        @pl.when(jnp.logical_and(t == CROSS_SLOT, mine < 2))
+        def _():
+            send_cross()
+
+        @pl.when(t == EARLY)
+        def _():
+            @pl.loop(0, 2)
+            def _(m):
+                update(m)
+
+        @pl.when(t == LATE + mine // 6 + mine // 7)
+        def _():
+            update(2)
+
+        late = LATE - 1 + mine // 7
+
+        @pl.when(jnp.logical_and(t >= late + 3, t < late + mats))
+        def _():
+            update(t - late)
+
+        @pl.when(t >= LATE + LAG_FWD)
+        def _():
+            forward(t - LATE - LAG_FWD)
 
         @pl.when(t == first_ns)
         def _():
             gather_x()
 
-            @pl.when(mine == GUARD)
+        begin = halves_before(t)
+        end = halves_before(t + 1)
+
+        @pl.loop(begin, jnp.minimum(end, 2 * NS_STEPS - 2))
+        def _(i):
+            @pl.when(i % 2 == 0)
             def _():
-                htp, hy = owner_of(HELD)
-                pl.semaphore_signal(s_go, inc=1, device_id={"tp": htp, "dp": hy * 2 + c}, device_id_type=MESH)
-
-        begin = steps_before(t)
-        end = steps_before(t + 1)
-
-        @pl.loop(begin, jnp.minimum(end, NS_STEPS - 1))
-        def _(i):
-            ns_step()
-
-        @pl.when(jnp.logical_and(begin < NS_STEPS, end == NS_STEPS))
+                ns_poly()
+
+            @pl.when(i % 2 == 1)
+            def _():
+                ns_apply()
+
+        @pl.when(jnp.logical_and(begin < 2 * NS_STEPS, end == 2 * NS_STEPS))
         def _():
             ns_last()
 
@@ -389,21 +419,22 @@
 
         otp, oyy = owner_of(j)
 
-        @pl.when(jnp.logical_and(mine != j, y == oyy))
+        direct = is_direct(j)
+
+        @pl.when(jnp.logical_or(jnp.logical_and(mine != j, y == oyy), jnp.logical_and(y != oyy, direct == 1)))
         def _():
             u_send(j, tp, dp_core).wait_send()
+
+        @pl.when(jnp.logical_and(jnp.logical_and(mine != j, y == oyy), direct == 0))
+        def _():
             u_pass(j, tp, dp_core).wait_send()
 
-        @pl.when(y != oyy)
+        @pl.when(jnp.logical_and(y != oyy, direct == 0))
         def _():
             u_cross(j).wait_send()
-        pltpu.make_async_copy(mom.at[j], mom_o.at[j], s_mo.at[j]).wait()
-        pltpu.make_async_copy(wt.at[j], wt_o.at[j], s_wo.at[j]).wait()
-        wb_local(j).wait()
         wb_core(j).wait_send()
         wb_core_in(j).wait_recv()
         wb_y(j).wait_send()
-        fwd_local(j).wait()
         fwd_core(j).wait_send()
         fwd_core_in(j).wait_recv()
     for q in range(2):
@@ -425,18 +456,17 @@
         dma = pltpu.SemaphoreType.DMA
         smem = pl.BlockSpec(memory_space=pltpu.SMEM)
         hbm = pl.BlockSpec(memory_space=pl.ANY)
+        vmem = pl.BlockSpec(memory_space=pltpu.VMEM)
         return pl.pallas_call(
             functools.partial(kernel, cfg),
-            out_shape=(jax.ShapeDtypeStruct((mats, rows, cols), F32),
-                       jax.ShapeDtypeStruct((mats, rows, cols), F32),
-                       jax.ShapeDtypeStruct((mats, nrow, cols), BF16)),
+            out_shape=(pltpu.VMEM((mats, rows, cols), F32),
+                       pltpu.VMEM((mats, rows, cols), F32),
+                       pltpu.VMEM((mats, nrow, cols), BF16)),
             in_specs=[smem, smem, hbm, hbm, hbm],
-            out_specs=(hbm, hbm, hbm),
+            out_specs=(vmem, vmem, vmem),
             scratch_shapes=[
                 pltpu.VMEM((mats, 2, rows, cols), F32),
                 pltpu.VMEM((mats, 2, rows, cols), F32),
-                pltpu.VMEM((mats, rows, cols), F32),
-                pltpu.VMEM((mats, rows, cols), F32),
                 pltpu.VMEM((mats, rows, cols), F32),
                 pltpu.VMEM((mats, rows, cols), BF16),
                 pltpu.VMEM((nrow, ncol), BF16),
@@ -445,8 +475,6 @@
                 pltpu.VMEM((mats, rows, cols), BF16),
                 pltpu.VMEM((16, cols), F32),
                 pltpu.VMEM((mats, rows, cols), BF16),
-                pltpu.VMEM((mats, rows, cols), BF16),
-                pltpu.VMEM((mats, rows, cols), BF16),
                 dma((mats, 2)), dma((mats,)), dma((mats,)),
                 dma((mats, 2)), dma((mats, 2)),
                 dma((mats,)), dma((mats,)),
@@ -454,13 +482,11 @@
                 dma((2, tp_size)), dma((2, tp_size)),
                 dma((2, tp_size)), dma((mats,)),
                 dma((mats,)), dma((mats,)), dma((mats,)),
-                dma((mats,)), dma((mats,)), dma((mats,)),
                 dma((mats,)), dma((mats,)), dma((mats,)), dma((mats,)),
-                dma((mats,)), dma((mats,)), dma((mats,)),
-                pltpu.SemaphoreType.REGULAR,
+                dma((mats,)), dma((mats,)),
             ],
             compiler_params=pltpu.CompilerParams(
-                collective_id=0, has_side_effects=True, vmem_limit_bytes=66 * 1024 * 1024 - 2 ** 21),
+                collective_id=0, has_side_effects=True, vmem_limit_bytes=VMEM_MIB * 2 ** 20),
             name="muon_step",
         )(learn_rate, decay_rate.reshape(1), grad_local[0], mom_local, weight_local)
 

time: 273 us -> 261 us (0.956); the launches traced: 273 us -> 257 us
  Pallas kernels: 256 us -> 248 us
  local copies, waits for them, and re-layouts: 15.2 us -> 8.12 us
    pallas_call x1, Pallas kernels: 256 us -> 248 us  [local_step(): pl.pallas_call(functools.partial(kernel, cfg), out_shape=(pltpu.VMEM((mat...]
    unnamed x5 -> x3, local copies, waits for them, and re-layouts: 15.2 us -> 8.12 us
where the time goes in v3:
time: 261 us; the launch traced here: 257 us
  Pallas kernels  248 us (95%)
  local copies, waits for them, and re-layouts  8.12 us (3%)
    pallas_call x1, Pallas kernels, local_step(): pl.pallas_call(functools.partial(kernel, cfg), out_shape=(pltpu.VMEM((mat...  248 us
    unnamed x3, local copies, waits for them, and re-layouts  8.12 us

profile of v3, /device:TPU:11, one launch (start us, length us, event | category | flops | bytes accessed | tf_op | source)
XLA Modules:
  0.0 256.9 jit_solution(15120120526095672941)
XLA Ops:
  1.3 247.5 %muon_step.1 = (f32[8,192,768]{2,1,0:T(8,128)S(1)}, f32[8,192,768]{2,1,0:T(8,128)S(1)}, bf16[8,768,768]{2,1,0:T(8,128)(2,1)S(1)}) custom-call(f32[8]{0:T(128)} %lr_ref.1, f32[1]{0:T(128)} %bitcast.2.decay_ref, f32[8,768,768]{2,1,0:T(8,128)} %bitcast.3, f32[8,192,768]{2,1,0:T(8,128)} %mom_in.1, f32[8,192,768]{2,1,0:T(8,128)} %wt_in.1), custom_call_target="tpu_custom_call" | custom-call | tf_op jit(solution)/shard_map/muon_step/pallas_call | solution.py:460
  248.8 2.2 copy.11
  251.0 2.2 copy.12
  253.2 3.7 %copy.13 = bf16[8,768,768]{2,1,0:T(8,128)(2,1)} copy(bf16[8,768,768]{2,1,0:T(8,128)(2,1)S(1)} %get-tuple-element.5) | data formatting | bytes 18874368

commit v4 on v3

--- a/solution.py
+++ b/solution.py
@@ -17,35 +17,38 @@
 F32 = jnp.float32
 BF16 = jnp.bfloat16
 
-OWNERS = ((2, 0), (1, 1), (3, 1), (0, 0), (0, 1), (3, 0), (1, 0), (2, 1))
-DIRECT = ()
-CROSS_SLOT = 9
+OWNERS = ((2, 0, 0), (1, 1, 0), (1, 0, 0), (2, 1, 0), (2, 0, 1), (1, 1, 1), (1, 0, 1), (2, 1, 1))
+NOBODY = 100
 AHEAD = 2
 VMEM_MIB = 44
 FAST_SLOTS = (6, 9)
+FIRST_NS = 3
+CROSS_SLOT = 9
 EARLY = 10
 LATE = 13
 LAG_FWD = 3
 
 
 def owner_of(j):
-    tp, y = 0, 0
-    for k, (tp_k, y_k) in enumerate(OWNERS):
+    tp, y, core = 0, 0, 0
+    for k, (tp_k, y_k, core_k) in enumerate(OWNERS):
         tp = tp + jnp.where(j == k, tp_k, 0)
         y = y + jnp.where(j == k, y_k, 0)
-    return tp, y
-
-
-def matrix_of(tp, y):
-    mine = 0
-    for k, (tp_k, y_k) in enumerate(OWNERS):
-        mine = mine + jnp.where(jnp.logical_and(tp == tp_k, y == y_k), k, 0)
+        core = core + jnp.where(j == k, core_k, 0)
+    return tp, y, y * 2 + core
+
+
+def matrix_of(tp, y, core):
+    mine = NOBODY
+    for k, (tp_k, y_k, core_k) in enumerate(OWNERS):
+        here = jnp.logical_and(tp == tp_k, jnp.logical_and(y == y_k, core == core_k))
+        mine = mine - jnp.where(here, NOBODY - k, 0)
     return mine
 
 
 def kernel(cfg, lr_ref, decay_ref, grad, mom_in, wt_in, mom, wt, wb,
            own, rcv, yr, ub, x, ga, gb, uf, acc, xr,
-           s_own, s_mom, s_wt, s_c2s, s_c2r, s_ys, s_yr, s_us, s_ur, s_fs, s_fr, s_xs, s_xr,
+           s_own, s_mom, s_wt, s_c2s, s_c2r, s_ys, s_yr, s_us, s_ur, s_xs, s_xr,
            s_hs, s_hr, s_vs, s_ps, s_pr, s_gs, s_gr, s_qs, s_qr):
     mats, rows, cols, ncol, out_scale, inv_dp = cfg
     full_rows = 4 * rows
@@ -57,7 +60,7 @@
     oc = 1 - c
     dp_core = y * 2 + oc
     dp_y = oy * 2 + c
-    mine = matrix_of(tp, y)
+    mine = matrix_of(tp, y, c)
 
     def rowq(q):
         return pl.ds(pl.multiple_of(q * rows, rows), rows)
@@ -83,12 +86,11 @@
         return remote(grad.at[j, rowq(q * 2 + oc), :], rcv.at[j, q], s_c2s.at[j, q], s_c2r.at[j, q], tp, dp_core)
 
     barrier = pltpu.get_barrier_semaphore()
-    pl.semaphore_signal(barrier, inc=1, device_id={"tp": tp, "dp": dp_core}, device_id_type=MESH)
-    for k in range(1, 8):
-        tgt = (tp * 2 + y + k) % 8
-        pl.semaphore_signal(barrier, inc=1, device_id={"tp": tgt // 2, "dp": (tgt % 2) * 2 + c}, device_id_type=MESH)
+    for k in range(1, 16):
+        tgt = (tp * 4 + dp + k) % 16
+        pl.semaphore_signal(barrier, inc=1, device_id={"tp": tgt // 4, "dp": tgt % 4}, device_id_type=MESH)
     own_copy(0, oy).start()
-    pl.semaphore_wait(barrier, 8)
+    pl.semaphore_wait(barrier, 15)
 
     def issue(j, first):
         core_send(j, oy).start()
@@ -114,14 +116,8 @@
             own[j, oy, rr, :] = own[j, oy, rr, :] + rcv[j, oy, rr, :]
         y_send(j).start()
 
-    def is_direct(j):
-        hit = 0
-        for k, tp_k, c_k in DIRECT:
-            hit = hit + jnp.where(jnp.logical_and(j == k, jnp.logical_and(tp == tp_k, c == c_k)), 1, 0)
-        return hit
-
     def u_send(j, tp_id, dp_id):
-        return remote(ub.at[j], x.at[rowq(dp), colq(tp)], s_us.at[j], s_ur.at[y, tp], tp_id, dp_id)
+        return remote(ub.at[j], x.at[rowq(dp), colq(tp)], s_us.at[j], s_ur.at[dp, tp], tp_id, dp_id)
 
     def sum_y(j):
         own_copy(j, y).wait()
@@ -137,7 +133,7 @@
             mom[j, rr, :] = m
             ub[j, rr, :] = (g + MOMENTUM * m).astype(BF16)
         wt_copy(j).start()
-        otp, oyy = owner_of(j)
+        otp, oyy, odp = owner_of(j)
 
         @pl.when(mine == j)
         def _():
@@ -145,15 +141,9 @@
 
         @pl.when(jnp.logical_and(mine != j, y == oyy))
         def _():
-            u_send(j, otp, dp).start()
-
-        direct = is_direct(j)
-
-        @pl.when(jnp.logical_and(y != oyy, direct == 1))
-        def _():
-            u_send(j, otp, oyy * 2 + c).start()
-
-        @pl.when(jnp.logical_and(y != oyy, direct == 0))
+            u_send(j, otp, odp).start()
+
+        @pl.when(y != oyy)
         def _():
             u_cross(j).start()
 
@@ -161,12 +151,12 @@
         return remote(ub.at[j], uf.at[j], s_hs.at[j], s_hr.at[j], tp, dp_y)
 
     def u_pass(j, tp_id, dp_id):
-        return remote(uf.at[j], x.at[rowq(dp_y), colq(tp)], s_vs.at[j], s_ur.at[oy, tp], tp_id, dp_id)
+        return remote(uf.at[j], x.at[rowq(dp_y), colq(tp)], s_vs.at[j], s_ur.at[dp_y, tp], tp_id, dp_id)
 
     def hop(j):
-        otp, oyy = owner_of(j)
-
-        @pl.when(jnp.logical_and(y == oyy, is_direct(j) == 0))
+        otp, oyy, odp = owner_of(j)
+
+        @pl.when(y == oyy)
         def _():
             u_cross(j).wait_recv()
 
@@ -176,18 +166,10 @@
 
             @pl.when(mine != j)
             def _():
-                u_pass(j, otp, dp).start()
-
-    def piece(yy, tt):
-        return remote(ub.at[0], x.at[rowq(yy * 2 + c), colq(tt)], s_us.at[0], s_ur.at[yy, tt], tp, dp_core)
-
-    def x_fwd(q, t):
-        blk = x.at[rowq(q * 2 + c), colq(t)]
-        return remote(blk, blk, s_fs.at[q, t], s_fr.at[q, t], tp, dp_core)
-
-    def x_fwd_in(q, t):
-        blk = x.at[rowq(q * 2 + oc), colq(t)]
-        return remote(blk, blk, s_fs.at[q, t], s_fr.at[q, t], tp, dp_core)
+                u_pass(j, otp, odp).start()
+
+    def piece(q, t):
+        return remote(ub.at[0], x.at[rowq(q), colq(t)], s_us.at[0], s_ur.at[q, t], tp, dp_core)
 
     def add_squares(q, t):
         def body(i, carry):
@@ -197,21 +179,15 @@
 
     def gather_x():
         acc[...] = jnp.zeros_like(acc)
-        for q in (y, oy):
-            for k in range(4):
+        for part, q in enumerate((dp, dp_core, dp_y, oy * 2 + oc)):
+            @pl.loop(0, 4)
+            def _(k):
                 t = (tp + k) % 4
-                if k > 0:
+
+                @pl.when(k >= 1 - part % 2)
+                def _():
                     piece(q, t).wait_recv()
-                x_fwd(q, t).start()
-                add_squares(q * 2 + c, t)
-        for q in (y, oy):
-            for k in range(4):
-                t = (tp + k) % 4
-                x_fwd_in(q, t).wait_recv()
-                add_squares(q * 2 + oc, t)
-        for q in range(2):
-            for t in range(4):
-                x_fwd(q, t).wait_send()
+                add_squares(q, t)
         total = jnp.sum(acc[...], axis=(0, 1), keepdims=True)
         inv = 1.0 / (jnp.sqrt(total) + NORM_EPS)
 
@@ -254,45 +230,40 @@
             x[:, rr] = (COEF_A * x[:, rr].astype(F32) + prod).astype(BF16)
 
     def ns_last():
-        gram()
-        for q in range(2):
-            part = ga[rowq(q * 2 + c), :]
-            sq = jnp.dot(part, ga[...], preferred_element_type=F32)
-            gb[q * rows:(q + 1) * rows, :] = (COEF_B * part.astype(F32) + COEF_C * sq).astype(BF16)
+        ns_poly()
 
         @pl.loop(0, 4)
         def _(i):
             t = i + (3 - 2 * i) * (1 - tp // 2)
-            prod = jnp.dot(gb[:2 * rows, :], x[:, colq(t)], preferred_element_type=F32)
-            for q in range(2):
-                rr = rowq(q * 2 + c)
-                x[rr, colq(t)] = (COEF_A * x[rr, colq(t)].astype(F32)
-                                  + prod[q * rows:(q + 1) * rows, :]).astype(BF16)
-            send_back(y, t)
+            prod = jnp.dot(gb[...], x[:, colq(t)], preferred_element_type=F32)
+            x[:, colq(t)] = (COEF_A * x[:, colq(t)].astype(F32) + prod).astype(BF16)
+            for k in range(2):
+                send_back(y * 2 + k, t)
 
         @pl.when(mine >= 2)
         def _():
             send_cross()
 
     def x_send(q, t):
-        return remote(x.at[rowq(q * 2 + c), colq(t)], xr.at[mine], s_xs.at[q, t], s_xr.at[mine], t, q * 2 + c)
+        return remote(x.at[rowq(q), colq(t)], xr.at[mine], s_xs.at[q, t], s_xr.at[mine], t, q)
 
     def x_recv(m):
         return remote(x.at[rowq(c), colq(0)], xr.at[m], s_xs.at[0, 0], s_xr.at[m], tp, dp_core)
 
     def send_back(q, t):
-        @pl.when(jnp.logical_or(y != q, tp != t))
+        @pl.when(jnp.logical_or(dp != q, tp != t))
         def _():
             x_send(q, t).start()
 
-        @pl.when(jnp.logical_and(y == q, tp == t))
-        def _():
-            xr[mine] = x[rowq(q * 2 + c), colq(t)]
+        @pl.when(jnp.logical_and(dp == q, tp == t))
+        def _():
+            xr[mine] = x[rowq(dp), colq(t)]
 
     def send_cross():
         @pl.loop(0, 4)
         def _(i):
-            send_back(oy, i + (3 - 2 * i) * (1 - tp // 2))
+            for k in range(2):
+                send_back(oy * 2 + k, i + (3 - 2 * i) * (1 - tp // 2))
 
     def wb_send(m, ss, rs, rows_id, dp_id):
         part = wb.at[m, rowq(rows_id), :]
@@ -338,7 +309,9 @@
         wb_y_in(m).wait_recv()
         fwd_core(m).start()
 
-    first_ns = mine + 4 - jnp.where(mine < 2, 1, 0)
+    first_ns = mine + FIRST_NS + jnp.where(mine > 5, 1, 0)
+    is_6 = jnp.where(mine == 6, 1, 0)
+    is_7 = jnp.where(mine == 7, 1, 0)
 
     def halves_before(t):
         done = 2 * (t - first_ns)
@@ -376,11 +349,11 @@
             def _(m):
                 update(m)
 
-        @pl.when(t == LATE + mine // 6 + mine // 7)
+        @pl.when(t == LATE + is_6 + 2 * is_7)
         def _():
             update(2)
 
-        late = LATE - 1 + mine // 7
+        late = LATE - 1 + is_7
 
         @pl.when(jnp.logical_and(t >= late + 3, t < late + mats))
         def _():
@@ -417,19 +390,14 @@
             core_send(j, q).wait_send()
         y_send(j).wait_send()
 
-        otp, oyy = owner_of(j)
-
-        direct = is_direct(j)
-
-        @pl.when(jnp.logical_or(jnp.logical_and(mine != j, y == oyy), jnp.logical_and(y != oyy, direct == 1)))
+        otp, oyy, odp = owner_of(j)
+
+        @pl.when(jnp.logical_and(mine != j, y == oyy))
         def _():
             u_send(j, tp, dp_core).wait_send()
-
-        @pl.when(jnp.logical_and(jnp.logical_and(mine != j, y == oyy), direct == 0))
-        def _():
             u_pass(j, tp, dp_core).wait_send()
 
-        @pl.when(jnp.logical_and(y != oyy, direct == 0))
+        @pl.when(y != oyy)
         def _():
             u_cross(j).wait_send()
         wb_core(j).wait_send()
@@ -437,11 +405,14 @@
         wb_y(j).wait_send()
         fwd_core(j).wait_send()
         fwd_core_in(j).wait_recv()
-    for q in range(2):
-        for t in range(4):
-            @pl.when(jnp.logical_or(y != q, tp != t))
-            def _():
-                x_send(q, t).wait_send()
+
+    @pl.when(mine < mats)
+    def _():
+        for q in range(4):
+            for t in range(4):
+                @pl.when(jnp.logical_or(dp != q, tp != t))
+                def _():
+                    x_send(q, t).wait_send()
 
 
 def solution(mesh):
@@ -478,9 +449,8 @@
                 dma((mats, 2)), dma((mats,)), dma((mats,)),
                 dma((mats, 2)), dma((mats, 2)),
                 dma((mats,)), dma((mats,)),
-                dma((mats,)), dma((2, tp_size)),
-                dma((2, tp_size)), dma((2, tp_size)),
-                dma((2, tp_size)), dma((mats,)),
+                dma((mats,)), dma((dp_size, tp_size)),
+                dma((dp_size, tp_size)), dma((mats,)),
                 dma((mats,)), dma((mats,)), dma((mats,)),
                 dma((mats,)), dma((mats,)), dma((mats,)), dma((mats,)),
                 dma((mats,)), dma((mats,)),

time: 261 us -> 246 us (0.943)
  Pallas kernels: 248 us -> 235 us
    pallas_call x1, Pallas kernels: 248 us -> 235 us  [local_step(): pl.pallas_call(functools.partial(kernel, cfg), out_shape=(pltpu.VMEM((mat...]
where the time goes in v4:
time: 246 us; the launch traced here: 245 us
  Pallas kernels  235 us (96%)
  local copies, waits for them, and re-layouts  8.12 us (3%)
    pallas_call x1, Pallas kernels, local_step(): pl.pallas_call(functools.partial(kernel, cfg), out_shape=(pltpu.VMEM((mat...  235 us
    unnamed x3, local copies, waits for them, and re-layouts  8.12 us

profile of v4, /device:TPU:11, one launch (start us, length us, event | category | flops | bytes accessed | tf_op | source)
XLA Modules:
  0.0 244.5 jit_solution(12433768099685070243)
XLA Ops:
  1.3 235.1 %muon_step.1 = (f32[8,192,768]{2,1,0:T(8,128)S(1)}, f32[8,192,768]{2,1,0:T(8,128)S(1)}, bf16[8,768,768]{2,1,0:T(8,128)(2,1)S(1)}) custom-call(f32[8]{0:T(128)} %lr_ref.1, f32[1]{0:T(128)} %bitcast.2.decay_ref, f32[8,768,768]{2,1,0:T(8,128)} %bitcast.3, f32[8,192,768]{2,1,0:T(8,128)} %mom_in.1, f32[8,192,768]{2,1,0:T(8,128)} %wt_in.1), custom_call_target="tpu_custom_call" | custom-call | tf_op jit(solution)/shard_map/muon_step/pallas_call | solution.py:431
  236.4 2.2 copy.11
  238.6 2.2 copy.12
  240.8 3.7 %copy.13 = bf16[8,768,768]{2,1,0:T(8,128)(2,1)} copy(bf16[8,768,768]{2,1,0:T(8,128)(2,1)S(1)} %get-tuple-element.5) | data formatting | bytes 18874368

commit v5 on v4

--- a/solution.py
+++ b/solution.py
@@ -312,6 +312,7 @@
     first_ns = mine + FIRST_NS + jnp.where(mine > 5, 1, 0)
     is_6 = jnp.where(mine == 6, 1, 0)
     is_7 = jnp.where(mine == 7, 1, 0)
+    early = EARLY + 2 * jnp.where(jnp.logical_and(mine >= 4, mine < 7), 1, 0)
 
     def halves_before(t):
         done = 2 * (t - first_ns)
@@ -343,7 +344,7 @@
         def _():
             send_cross()
 
-        @pl.when(t == EARLY)
+        @pl.when(t == early)
         def _():
             @pl.loop(0, 2)
             def _(m):

time: 246 us -> 243 us (0.988)
  no operation moved by 1% of the time
where the time goes in v5:
time: 243 us
  Pallas kernels  233 us (96%)
  local copies, waits for them, and re-layouts  8.12 us (3%)
    pallas_call x1, Pallas kernels, local_step(): pl.pallas_call(functools.partial(kernel, cfg), out_shape=(pltpu.VMEM((mat...  233 us
    unnamed x3, local copies, waits for them, and re-layouts  8.12 us

profile of v5, /device:TPU:11, one launch (start us, length us, event | category | flops | bytes accessed | tf_op | source)
XLA Modules:
  0.0 242.5 jit_solution(6912503396094278168)
XLA Ops:
  1.3 233.1 %muon_step.1 = (f32[8,192,768]{2,1,0:T(8,128)S(1)}, f32[8,192,768]{2,1,0:T(8,128)S(1)}, bf16[8,768,768]{2,1,0:T(8,128)(2,1)S(1)}) custom-call(f32[8]{0:T(128)} %lr_ref.1, f32[1]{0:T(128)} %bitcast.2.decay_ref, f32[8,768,768]{2,1,0:T(8,128)} %bitcast.3, f32[8,192,768]{2,1,0:T(8,128)} %mom_in.1, f32[8,192,768]{2,1,0:T(8,128)} %wt_in.1), custom_call_target="tpu_custom_call" | custom-call | tf_op jit(solution)/shard_map/muon_step/pallas_call | solution.py:432
  234.4 2.2 copy.11
  236.6 2.2 copy.12
  238.8 3.7 %copy.13 = bf16[8,768,768]{2,1,0:T(8,128)(2,1)} copy(bf16[8,768,768]{2,1,0:T(8,128)(2,1)S(1)} %get-tuple-element.5) | data formatting | bytes 18874368
